TPU v7x, 32 devices: a whole 2x2x4 slice. The times are simulated.
32 devices in a mesh: shard: 4 (over y, x), ctx: 2 (over core), tp: 4 (over z).
Axes of the slice: x: 2, y: 2, z: 4, core: 2. Of those that a mesh axis runs over, the one named last changes fastest.
Arguments:
- tokens: bfloat16 [4, 2048, 2048], P('shard', 'ctx'), may hold values from -6 to 6
- lengths: int32 [4], P('shard'), may hold values from 512 to 2048, as said below
- cotangent: bfloat16 [4, 2048, 2048], P('shard', 'ctx'), may hold values from -6 to 6
- w_query: float32 [2048, 2048], P(('shard', 'ctx'), 'tp'), may hold values from -0.1875 to 0.1875
- w_key: float32 [2048, 2048], P(('shard', 'ctx'), 'tp'), may hold values from -0.1875 to 0.1875
- w_value: float32 [2048, 2048], P(('shard', 'ctx'), 'tp'), may hold values from -0.125 to 0.125
- w_output: float32 [2048, 2048], P('tp', ('shard', 'ctx')), may hold values from -1 to 1
- w_gate: float32 [2048, 8192], P(('shard', 'ctx'), 'tp'), may hold values from -0.125 to 0.125
- w_up: float32 [2048, 8192], P(('shard', 'ctx'), 'tp'), may hold values from -0.125 to 0.125
- w_down: float32 [8192, 2048], P('tp', ('shard', 'ctx')), may hold values from -0.0625 to 0.0625
Outputs:
- output: bfloat16 [4, 2048, 2048], P('shard', 'ctx')
- grad_tokens: float32 [4, 2048, 2048], P('shard', 'ctx')
- grad_query: float32 [2048, 2048], P(('shard', 'ctx'), 'tp')
- grad_key: float32 [2048, 2048], P(('shard', 'ctx'), 'tp')
- grad_value: float32 [2048, 2048], P(('shard', 'ctx'), 'tp')
- grad_output: float32 [2048, 2048], P('tp', ('shard', 'ctx'))
- grad_gate: float32 [2048, 8192], P(('shard', 'ctx'), 'tp')
- grad_up: float32 [2048, 8192], P(('shard', 'ctx'), 'tp')
- grad_down: float32 [8192, 2048], P('tp', ('shard', 'ctx'))
Inputs may be any that keep to these rules, and one draw needn't show every extreme that they name: Slots 0 to lengths[b] - 1 of sequence b are valid, the rest padding; some sequence is full and some has 512 valid slots.
All inputs are finite; a program needn't handle non-finite values.
Results may differ from a plain program's by a relative error of at most 0.014.
The roundings to bfloat16 on the way count: a program that leaves them out, or rounds other values in their place, can miss the bound.
Values may be sent and summed in bfloat16 or wider, within the bound.
A program may use at most 256 MiB of HBM per device.

v0:
```python
import jax
import jax.numpy as jnp
from jax import lax
from jax.sharding import PartitionSpec as P

HEAD_DIM = 128
EPSILON = 1e-05


def normalize(values):
    center = values - jnp.mean(values, axis=-1, keepdims=True)
    inv_scale = lax.rsqrt(jnp.mean(center * center, axis=-1, keepdims=True) + EPSILON)
    return (center * inv_scale, inv_scale)


def norm_back(normed, inv_scale, upstream):
    first_mean = jnp.mean(upstream, axis=-1, keepdims=True)
    second_mean = jnp.mean(upstream * normed, axis=-1, keepdims=True)
    return inv_scale * (upstream - first_mean - normed * second_mean)


def rope_tables(row_count, head_size, offset):
    positions = (jnp.arange(row_count) + offset).astype(jnp.float32)
    inverse = 10000.0 ** (-(jnp.arange(head_size // 2).astype(jnp.float32) * 2.0) / head_size)
    angles = positions[:, None] * inverse[None, :]
    angles = jnp.concatenate([angles, angles], axis=-1)
    return (jnp.cos(angles)[:, None, :], jnp.sin(angles)[:, None, :])


def turn_half(values):
    half_dim = values.shape[-1] // 2
    return jnp.concatenate([-values[..., half_dim:], values[..., :half_dim]], axis=-1)


def rotate(values, cosine, sine_table):
    return values * cosine + turn_half(values) * sine_table


def rotate_back(values, cosine, sine_table):
    return values * cosine - turn_half(values) * sine_table


def score_block(query_rows, keys_seq, length, row_start):
    block_rows = query_rows.shape[0]
    key_pos = jnp.arange(keys_seq.shape[0])
    row_pos = row_start + jnp.arange(block_rows)
    scores = jnp.einsum(
        "qhd,khd->hqk", query_rows, keys_seq, preferred_element_type=jnp.float32
    ) * HEAD_DIM ** (-0.5)
    allowed = (key_pos[None, :] <= row_pos[:, None]) & (key_pos[None, :] < length)
    return jnp.where(allowed[None], scores, -1e30)


def attend_forward(queries_seq, keys_seq, values_seq, length, offset):
    half_len, head_count, head_size = queries_seq.shape
    block_rows = min(512, half_len)
    block_count = half_len // block_rows
    grouped = queries_seq.reshape(block_count, block_rows, head_count, head_size)

    def one_block(paired):
        query_rows, block_index = paired
        scores = score_block(query_rows, keys_seq, length, offset + block_index * block_rows)
        row_peak = jnp.max(scores, axis=-1, keepdims=True)
        log_total = jnp.log(jnp.sum(jnp.exp(scores - row_peak), axis=-1, keepdims=True)) + row_peak
        probability = jnp.exp(scores - log_total).astype(jnp.bfloat16)
        attended = jnp.einsum(
            "hqk,khd->qhd", probability, values_seq, preferred_element_type=jnp.float32
        )
        return (attended.astype(jnp.bfloat16), log_total[..., 0])

    attended, log_totals = lax.map(one_block, (grouped, jnp.arange(block_count)))
    return (attended.reshape(half_len, head_count, head_size), log_totals)


def attend_backward(queries_seq, keys_seq, values_seq, length, offset, log_totals, grad_seq):
    half_len, head_count, head_size = queries_seq.shape
    block_rows = min(512, half_len)
    block_count = half_len // block_rows
    score_scale = HEAD_DIM ** (-0.5)
    grouped = queries_seq.reshape(block_count, block_rows, head_count, head_size)
    grad_grouped = grad_seq.reshape(block_count, block_rows, head_count, head_size)

    def one_block(carried, paired):
        query_rows, grad_rows, log_rows, block_index = paired
        scores = score_block(query_rows, keys_seq, length, offset + block_index * block_rows)
        probability = jnp.exp(scores - log_rows[..., None])
        prob_low = probability.astype(jnp.bfloat16)
        grad_prob = jnp.einsum(
            "qhd,khd->hqk", grad_rows, values_seq, preferred_element_type=jnp.float32
        )
        inner_sum = jnp.sum(probability * grad_prob, axis=-1, keepdims=True)
        grad_scores = (probability * (grad_prob - inner_sum)).astype(jnp.bfloat16)
        grad_query_rows = (
            jnp.einsum("hqk,khd->qhd", grad_scores, keys_seq, preferred_element_type=jnp.float32)
            * score_scale
        )
        key_part = (
            jnp.einsum("hqk,qhd->khd", grad_scores, query_rows, preferred_element_type=jnp.float32)
            * score_scale
        )
        value_part = jnp.einsum(
            "hqk,qhd->khd", prob_low, grad_rows, preferred_element_type=jnp.float32
        )
        return ((carried[0] + key_part, carried[1] + value_part), grad_query_rows)

    empty = jnp.zeros(keys_seq.shape, jnp.float32)
    sums, grad_queries = lax.scan(
        one_block, (empty, empty), (grouped, grad_grouped, log_totals, jnp.arange(block_count))
    )
    return (grad_queries.reshape(half_len, head_count, head_size), sums[0], sums[1])


def matmul_low(left, right):
    return jnp.dot(left, right, preferred_element_type=jnp.float32)


def body(tokens, lengths, cotangent, w_query, w_key, w_value, w_output, w_gate, w_up, w_down):
    seq_count, half_len, model_width = tokens.shape
    head_cols = w_query.shape[1]
    head_count = head_cols // HEAD_DIM
    row_total = seq_count * half_len
    offset = lax.axis_index("ctx") * half_len
    positions = offset + jnp.arange(half_len)
    valid_mask = (positions[None, :] < lengths[:, None]).astype(jnp.float32)
    bf_type = jnp.bfloat16
    attn_low = (
        w_query.astype(bf_type),
        w_key.astype(bf_type),
        w_value.astype(bf_type),
        w_output.astype(bf_type),
    )
    mlp_low = (w_gate.astype(bf_type), w_up.astype(bf_type), w_down.astype(bf_type))
    query_full, key_full, value_full, output_full = (
        lax.all_gather(attn_low[0], ("shard", "ctx"), axis=0, tiled=True),
        lax.all_gather(attn_low[1], ("shard", "ctx"), axis=0, tiled=True),
        lax.all_gather(attn_low[2], ("shard", "ctx"), axis=0, tiled=True),
        lax.all_gather(attn_low[3], ("shard", "ctx"), axis=1, tiled=True),
    )
    gate_full, up_full, down_full = (
        lax.all_gather(mlp_low[0], ("shard", "ctx"), axis=0, tiled=True),
        lax.all_gather(mlp_low[1], ("shard", "ctx"), axis=0, tiled=True),
        lax.all_gather(mlp_low[2], ("shard", "ctx"), axis=1, tiled=True),
    )
    tokens_wide = tokens.astype(jnp.float32).reshape(row_total, model_width)
    normed_one, scale_one = normalize(tokens_wide)
    input_one = normed_one.astype(bf_type)
    split_heads = (seq_count, half_len, head_count, HEAD_DIM)
    query_pre = matmul_low(input_one, query_full).reshape(split_heads)
    key_pre = matmul_low(input_one, key_full).reshape(split_heads)
    value_pre = matmul_low(input_one, value_full).reshape(split_heads)
    cosine, sine_table = rope_tables(half_len, HEAD_DIM, offset)
    queries = rotate(query_pre, cosine, sine_table).astype(bf_type)
    keys_rot = rotate(key_pre, cosine, sine_table).astype(bf_type)
    values_low = value_pre.astype(bf_type)
    keys_all, values_all = (
        lax.all_gather(keys_rot, "ctx", axis=1, tiled=True),
        lax.all_gather(values_low, "ctx", axis=1, tiled=True),
    )
    seq_index = 0
    attended, log_totals = attend_forward(
        queries[seq_index], keys_all[seq_index], values_all[seq_index], lengths[seq_index], offset
    )
    attended_list = [attended]
    log_list = [log_totals]
    attn_out = jnp.stack(attended_list).reshape(row_total, head_cols)
    branch_part = matmul_low(attn_out, output_full)
    resid = tokens_wide + lax.psum(branch_part, "tp")
    normed_two, scale_two = normalize(resid)
    input_two = normed_two.astype(bf_type)
    gate_proj = matmul_low(input_two, gate_full)
    up_proj = matmul_low(input_two, up_full)
    gate_sigmoid = jax.nn.sigmoid(gate_proj)
    hidden = (gate_proj * gate_sigmoid * up_proj).astype(bf_type)
    branch_two_part = matmul_low(hidden, down_full)
    final_sum = resid + lax.psum(branch_two_part.astype(jnp.bfloat16), "tp").astype(jnp.float32)
    grad_final = cotangent.astype(jnp.float32).reshape(row_total, model_width) * valid_mask.reshape(
        row_total, 1
    )
    grad_branch = grad_final.astype(bf_type)
    grad_down = jnp.einsum("rf,rd->fd", hidden, grad_branch, preferred_element_type=jnp.float32)
    grad_hidden = jnp.einsum(
        "rd,fd->rf", grad_branch, down_full, preferred_element_type=jnp.float32
    )
    grad_gate_act = (
        grad_hidden * up_proj * gate_sigmoid * (1.0 + gate_proj * (1.0 - gate_sigmoid))
    ).astype(bf_type)
    grad_up_act = (grad_hidden * gate_proj * gate_sigmoid).astype(bf_type)
    grad_gate = jnp.einsum(
        "rd,rf->df", input_two, grad_gate_act, preferred_element_type=jnp.float32
    )
    grad_up = jnp.einsum("rd,rf->df", input_two, grad_up_act, preferred_element_type=jnp.float32)
    grad_input_two = jnp.einsum(
        "rf,df->rd", grad_gate_act, gate_full, preferred_element_type=jnp.float32
    ) + jnp.einsum("rf,df->rd", grad_up_act, up_full, preferred_element_type=jnp.float32)
    mlp_grads = (
        lax.psum_scatter(grad_gate, ("shard", "ctx"), scatter_dimension=0, tiled=True),
        lax.psum_scatter(grad_up, ("shard", "ctx"), scatter_dimension=0, tiled=True),
        lax.psum_scatter(grad_down, ("shard", "ctx"), scatter_dimension=1, tiled=True),
    )
    grad_input_two = lax.psum(grad_input_two, "tp")
    grad_resid = grad_final + norm_back(normed_two, scale_two, grad_input_two)
    grad_resid_low = grad_resid.astype(bf_type)
    grad_wout = jnp.einsum(
        "rc,rd->cd", attn_out, grad_resid_low, preferred_element_type=jnp.float32
    )
    grad_attn = jnp.einsum(
        "rd,cd->rc", grad_resid_low, output_full, preferred_element_type=jnp.float32
    )
    grad_attn = grad_attn.astype(bf_type).reshape(split_heads)
    seq_index = 0
    grad_queries, grad_keys_seq, grad_values_seq = attend_backward(
        queries[seq_index],
        keys_all[seq_index],
        values_all[seq_index],
        lengths[seq_index],
        offset,
        log_list[seq_index],
        grad_attn[seq_index],
    )
    query_grads = [grad_queries]
    key_grads = [grad_keys_seq]
    value_grads = [grad_values_seq]
    grad_keys, grad_values = (
        lax.psum_scatter(jnp.stack(key_grads), "ctx", scatter_dimension=1, tiled=True),
        lax.psum_scatter(jnp.stack(value_grads), "ctx", scatter_dimension=1, tiled=True),
    )
    grad_q_pre = (
        rotate_back(jnp.stack(query_grads), cosine, sine_table)
        .astype(bf_type)
        .reshape(row_total, head_cols)
    )
    grad_k_pre = (
        rotate_back(grad_keys, cosine, sine_table).astype(bf_type).reshape(row_total, head_cols)
    )
    grad_v_pre = grad_values.astype(bf_type).reshape(row_total, head_cols)
    grad_wq = jnp.einsum("rd,rc->dc", input_one, grad_q_pre, preferred_element_type=jnp.float32)
    grad_wk = jnp.einsum("rd,rc->dc", input_one, grad_k_pre, preferred_element_type=jnp.float32)
    grad_wv = jnp.einsum("rd,rc->dc", input_one, grad_v_pre, preferred_element_type=jnp.float32)
    grad_input_one = (
        jnp.einsum("rc,dc->rd", grad_q_pre, query_full, preferred_element_type=jnp.float32)
        + jnp.einsum("rc,dc->rd", grad_k_pre, key_full, preferred_element_type=jnp.float32)
        + jnp.einsum("rc,dc->rd", grad_v_pre, value_full, preferred_element_type=jnp.float32)
    )
    attn_grads = (
        lax.psum_scatter(grad_wq, ("shard", "ctx"), scatter_dimension=0, tiled=True),
        lax.psum_scatter(grad_wk, ("shard", "ctx"), scatter_dimension=0, tiled=True),
        lax.psum_scatter(grad_wv, ("shard", "ctx"), scatter_dimension=0, tiled=True),
        lax.psum_scatter(grad_wout, ("shard", "ctx"), scatter_dimension=1, tiled=True),
    )
    grad_input_one = lax.psum(grad_input_one, "tp")
    grad_tokens = grad_resid + norm_back(normed_one, scale_one, grad_input_one)
    output = final_sum.astype(bf_type).reshape(seq_count, half_len, model_width)
    grad_tokens = grad_tokens.reshape(seq_count, half_len, model_width)
    return (
        output,
        grad_tokens,
        attn_grads[0],
        attn_grads[1],
        attn_grads[2],
        attn_grads[3],
        mlp_grads[0],
        mlp_grads[1],
        mlp_grads[2],
    )


def solution(mesh):
    return jax.shard_map(
        body,
        mesh=mesh,
        in_specs=(
            P("shard", "ctx", None),
            P("shard"),
            P("shard", "ctx", None),
            P(("shard", "ctx"), "tp"),
            P(("shard", "ctx"), "tp"),
            P(("shard", "ctx"), "tp"),
            P("tp", ("shard", "ctx")),
            P(("shard", "ctx"), "tp"),
            P(("shard", "ctx"), "tp"),
            P("tp", ("shard", "ctx")),
        ),
        out_specs=(
            P("shard", "ctx", None),
            P("shard", "ctx", None),
            P(("shard", "ctx"), "tp"),
            P(("shard", "ctx"), "tp"),
            P(("shard", "ctx"), "tp"),
            P("tp", ("shard", "ctx")),
            P(("shard", "ctx"), "tp"),
            P(("shard", "ctx"), "tp"),
            P("tp", ("shard", "ctx")),
        ),
        check_vma=False,
    )
```

profile of v0, /device:TPU:0, one launch (start us, length us, event | category | flops | bytes accessed | tf_op | source)
XLA Modules:
  0.0 2208.8 jit_solution(8768566741574588461)
XLA Ops:
  14.8 3.2 convert_reduce_fusion
  21.9 19.1 all-gather.13.cloned.1.call-done
  41.0 5.2 fusion.107
  48.2 23.1 %all-gather.17.cloned.1.call-done = bf16[2048,512]{1,0:T(8,128)(2,1)} async-done(((bf16[256,512]{1,0:T(8,128)(2,1)}), bf16[2048,512]{1,0:T(8,128)(2,1)}) %all-gather.17.cloned.1.call-update) | async-done | bytes 2097168 | tf_op jit(solution)/shard_map/all_gather | solution.py:136
  74.2 5.6 fusion.79
  83.4 18.1 all-gather.11.cloned.1.call-done
  101.5 6.6 fusion.106
  111.2 3.3 slice_negate_fusion.3
  128.5 4.5 fusion.61
  136.1 35.1 %while.27 = (s32[]{:T(128)}, bf16[2,512,4,128]{3,2,1,0:T(4,128)(2,1)S(1)}, f32[2,4,512]{2,1,0:T(4,128)S(1)}, s32[2]{0:T(128)S(1)}, s32[]{:T(128)}, /*index=5*/s3...) while((s32[]{:T(128)}, ...), condition=%wide.region_5.6_spmd, body=%wide.region_2.5_spmd.sunk | while | flops 2195980800 | bytes 69280448 | solution.py:71
  139.2 4.5 fusion.170
  143.7 4.4 exponential_reduce_fusion.2
  148.1 5.3 fusion.171
  156.6 4.5 fusion.170
  161.0 4.4 exponential_reduce_fusion.2
  165.5 5.3 fusion.171
  171.3 8.4 fusion.87
  187.3 283.6 %all-reduce.5.cloned.1.call-done = f32[1024,2048]{1,0:T(8,128)} async-done(((f32[1024,2048]{1,0:T(8,128)}), f32[1024,2048]{1,0:T(8,128)}) %all-reduce.5.cloned.1.call-update) | async-done | bytes 8388624 | tf_op jit(solution)/shard_map/psum | solution.py:167
  470.9 5.5 fusion.104
  482.5 44.2 %all-gather.21.cloned.1.call-done = bf16[2048,2048]{1,0:T(8,128)(2,1)} async-done(((bf16[256,2048]{1,0:T(8,128)(2,1)}), bf16[2048,2048]{1,0:T(8,128)(2,1)}) %all-gather.21.cloned.1.call-update) | async-done | bytes 8388624 | tf_op jit(solution)/shard_map/all_gather | solution.py:140
  526.6 14.5 fusion.108
  541.1 42.3 %all-gather.23.cloned.1.call-done = bf16[2048,2048]{1,0:T(8,128)(2,1)} async-done(((bf16[256,2048]{1,0:T(8,128)(2,1)}), bf16[2048,2048]{1,0:T(8,128)(2,1)}) %all-gather.23.cloned.1.call-update) | async-done | bytes 8388624 | tf_op jit(solution)/shard_map/all_gather | solution.py:141
  583.4 14.4 fusion.109
  597.8 43.8 %all-gather.25.cloned.1.call-done = bf16[2048,2048]{1,0:T(8,128)(2,1)} async-done(((bf16[2048,256]{1,0:T(8,128)(2,1)}), bf16[2048,2048]{1,0:T(8,128)(2,1)}) %all-gather.25.cloned.1.call-update) | async-done | bytes 8388624 | tf_op jit(solution)/shard_map/all_gather | solution.py:142
  641.6 22.0 multiply_convert_fusion.1
  663.6 15.1 fusion.110
  678.8 13.0 convolution_add_fusion
  691.8 13.8 convolution_convert_fusion
  705.7 277.0 %all-reduce.9.cloned.1.call-done = f32[1024,2048]{1,0:T(8,128)} async-done(((f32[1024,2048]{1,0:T(8,128)}), f32[1024,2048]{1,0:T(8,128)}) %all-reduce.9.cloned.1.call-update) | async-done | bytes 8388624 | tf_op jit(solution)/shard_map/psum | solution.py:200
  982.7 6.8 fusion.103
  989.6 149.9 %all-reduce.7.cloned.1.call-done = bf16[1024,2048]{1,0:T(8,128)(2,1)} async-done(((bf16[1024,2048]{1,0:T(8,128)(2,1)}), bf16[1024,2048]{1,0:T(8,128)(2,1)}) %all-reduce.7.cloned.1.call-update) | async-done | bytes 4194320 | tf_op jit(solution)/shard_map/psum | solution.py:175
  1139.5 12.3 fusion.46
  1151.9 3.4 copy-done.7
  1158.7 129.7 %while.28 = (s32[]{:T(128)}, f32[2048,4,128]{0,2,1:T(8,128)}, f32[2048,4,128]{0,2,1:T(8,128)}, f32[2,512,4,128]{3,1,2,0:T(8,128)}, bf16[2,512,4,128]{3,1,2,0:T(8...) while((s32[]{:T(128)}, f32[2048,4,128]{0,2,1:T(8,128)}, ...), condition=%wide.region_15.16_spmd.clone, body=%wide.region_13.15_spmd.clone.sunk | while | flops 5439226368 | bytes 211879280 | solution.py:107
  1158.9 9.2 fusion.180
  1172.0 13.1 multiply_reduce_fusion.4
  1185.2 14.9 multiply_convert_fusion.5
  1200.1 7.5 bitcast_add_fusion.4
  1211.3 11.0 bitcast_add_fusion.5
  1222.3 9.2 fusion.180
  1235.4 13.1 multiply_reduce_fusion.4
  1248.6 14.9 multiply_convert_fusion.5
  1263.5 8.7 bitcast_add_fusion.4
  1275.9 12.2 bitcast_add_fusion.5
  1296.5 5.6 fusion.82
  1306.0 6.6 fusion.111
  1317.8 11.7 add_add_fusion
  1333.6 5.2 fusion.54
  1340.0 7.8 fusion.68
  1349.0 7.0 fusion.52
  1357.2 7.1 fusion.56
  1364.4 15.3 fusion.112
  1379.8 15.2 fusion.113
  1395.6 15.6 fusion.72
  1411.3 210.5 %all-reduce.11.cloned.1.call-done = f32[1024,2048]{1,0:T(8,128)} async-done(((f32[1024,2048]{1,0:T(8,128)}), f32[1024,2048]{1,0:T(8,128)}) %all-reduce.11.cloned.1.call-update) | async-done | bytes 8388624 | tf_op jit(solution)/shard_map/psum | solution.py:250
  1621.8 6.8 fusion.102
  1630.2 7.5 fusion.42
  1637.7 38.1 %reduce-scatter.14.cloned.1.call-done = f32[256,512]{1,0:T(8,128)} async-done(((f32[2048,512]{1,0:T(8,128)}), f32[256,512]{1,0:T(8,128)}) %reduce-scatter.14.cloned.1.call-update) | async-done | bytes 524304 | tf_op jit(solution)/shard_map/reduce_scatter | solution.py:245
  1675.8 54.9 %reduce-scatter.20.cloned.1.call-done = f32[512,256]{1,0:T(8,128)} async-done(((f32[512,2048]{1,0:T(8,128)}), f32[512,256]{1,0:T(8,128)}) %reduce-scatter.20.cloned.1.call-update) | async-done | bytes 524304 | tf_op jit(solution)/shard_map/reduce_scatter | solution.py:248
  1730.7 55.0 %reduce-scatter.16.cloned.1.call-done = f32[256,512]{1,0:T(8,128)} async-done(((f32[2048,512]{1,0:T(8,128)}), f32[256,512]{1,0:T(8,128)}) %reduce-scatter.16.cloned.1.call-update) | async-done | bytes 524304 | tf_op jit(solution)/shard_map/reduce_scatter | solution.py:246
  1785.7 55.1 %reduce-scatter.18.cloned.1.call-done = f32[256,512]{1,0:T(8,128)} async-done(((f32[2048,512]{1,0:T(8,128)}), f32[256,512]{1,0:T(8,128)}) %reduce-scatter.18.cloned.1.call-update) | async-done | bytes 524304 | tf_op jit(solution)/shard_map/reduce_scatter | solution.py:247
  1840.8 120.2 %reduce-scatter.22.cloned.1.call-done = f32[256,2048]{1,0:T(8,128)} async-done(((f32[2048,2048]{1,0:T(8,128)}), f32[256,2048]{1,0:T(8,128)}) %reduce-scatter.22.cloned.1.call-update) | async-done | bytes 2097168 | tf_op jit(solution)/shard_map/reduce_scatter | solution.py:196
  1961.0 120.4 %reduce-scatter.24.cloned.1.call-done = f32[256,2048]{1,0:T(8,128)} async-done(((f32[2048,2048]{1,0:T(8,128)}), f32[256,2048]{1,0:T(8,128)}) %reduce-scatter.24.cloned.1.call-update) | async-done | bytes 2097168 | tf_op jit(solution)/shard_map/reduce_scatter | solution.py:197
  2081.4 120.2 %reduce-scatter.26.cloned.1.call-done = f32[2048,256]{1,0:T(8,128)} async-done(((f32[2048,2048]{1,0:T(8,128)}), f32[2048,256]{1,0:T(8,128)}) %reduce-scatter.26.cloned.1.call-update) | async-done | bytes 2097168 | tf_op jit(solution)/shard_map/reduce_scatter | solution.py:198
  (245 shorter events, 102.2 us)
Async XLA Ops:
  7.2 33.8 %all-gather.13.cloned.1.call-start = ((), (), s32[]{:S(2)}) async-start(), calls=%async_computation.10 | async-start | bytes 2359296 | tf_op jit(solution)/shard_map/all_gather | solution.py:135
  9.0 62.2 %all-gather.17.cloned.1.call-start = ((), (), s32[]{:S(2)}) async-start(), calls=%async_computation.12 | async-start | bytes 2359296 | tf_op jit(solution)/shard_map/all_gather | solution.py:136
  10.9 90.7 %all-gather.11.cloned.1.call-start = ((), (), s32[]{:S(2)}) async-start(), calls=%async_computation.9 | async-start | bytes 2359296 | tf_op jit(solution)/shard_map/all_gather | solution.py:134
  12.7 120.2 %all-gather.15.cloned.1.call-start = ((), (), s32[]{:S(2)}) async-start(), calls=%async_computation.11 | async-start | bytes 3145728 | tf_op jit(solution)/shard_map/all_gather | solution.py:156
  12.8 5.2 copy-start.4
  14.8 31.7 %copy-start.17 = (f32[1024,128]{0,1:T(8,128)}, f32[1024,128]{0,1:T(8,128)S(1)}, u32[]{:S(2)}) copy-start(f32[1024,128]{0,1:T(8,128)S(1)} %get-tuple-element.318) | copy-start | bytes 1572868
  14.8 31.7 %copy-start.19 = (f32[1024,128]{0,1:T(8,128)}, f32[1024,128]{0,1:T(8,128)S(1)}, u32[]{:S(2)}) copy-start(f32[1024,128]{0,1:T(8,128)S(1)} %get-tuple-element.319) | copy-start | bytes 1572868
  18.0 56.2 %copy-start.38 = (f32[1024]{0:T(1024)}, f32[1024]{0:T(1024)S(1)}, u32[]{:S(2)}) copy-start(f32[1024]{0:T(1024)S(1)} %broadcast_multiply_fusion.7) | copy-start | bytes 12292
  19.3 54.9 %copy-start.42 = (f32[1024]{0:T(1024)}, f32[1024]{0:T(1024)S(1)}, u32[]{:S(2)}) copy-start(f32[1024]{0:T(1024)S(1)} %add_rsqrt_fusion.1) | copy-start | bytes 12292
  48.1 87.9 %all-gather.27.cloned.1.call-start = ((), (), s32[]{:S(2)}) async-start(), calls=%async_computation.30 | async-start | bytes 3145728 | tf_op jit(solution)/shard_map/all_gather | solution.py:157
  74.2 5.7 copy-start.37
  79.9 91.4 %all-gather.19.cloned.1.call-start = ((), (), s32[]{:S(2)}) async-start(), calls=%async_computation.13 | async-start | bytes 2359296 | tf_op jit(solution)/shard_map/all_gather | solution.py:137
  80.7 390.2 %all-reduce.5.cloned.1.call-start = ((), (), s32[]{:S(2)}) async-start(), calls=%async_computation.14 | async-start | bytes 16777216 | tf_op jit(solution)/shard_map/psum | solution.py:167
  83.4 45.1 %copy-start.21 = (f32[2,512,128]{2,1,0:T(8,128)}, f32[2,512,128]{2,1,0:T(8,128)S(1)}, u32[]{:S(2)}) copy-start(f32[2,512,128]{2,1,0:T(8,128)S(1)} %get-tuple-element.316) | copy-start | bytes 1572868
  83.4 45.0 %copy-start.23 = (f32[2,512,128]{2,1,0:T(8,128)}, f32[2,512,128]{2,1,0:T(8,128)S(1)}, u32[]{:S(2)}) copy-start(f32[2,512,128]{2,1,0:T(8,128)S(1)} %get-tuple-element.317) | copy-start | bytes 1572868
  132.9 3.2 copy-start.34
  143.7 4.4 copy-start.10
  161.0 4.4 copy-start.10
  171.2 8.5 copy-start.1
  171.2 8.5 copy-start.35
  171.3 8.5 copy-start.40
  179.8 346.9 %all-gather.21.cloned.1.call-start = ((), (), s32[]{:S(2)}) async-start(), calls=%async_computation.15 | async-start | bytes 9437184 | tf_op jit(solution)/shard_map/all_gather | solution.py:140
  182.4 3.0 copy-start.30
  182.5 400.9 %all-gather.23.cloned.1.call-start = ((), (), s32[]{:S(2)}) async-start(), calls=%async_computation.16 | async-start | bytes 9437184 | tf_op jit(solution)/shard_map/all_gather | solution.py:141
  185.4 456.2 %all-gather.25.cloned.1.call-start = ((), (), s32[]{:S(2)}) async-start(), calls=%async_computation.17 | async-start | bytes 9437184 | tf_op jit(solution)/shard_map/all_gather | solution.py:142
  186.6 796.2 %all-reduce.9.cloned.1.call-start = ((), (), s32[]{:S(2)}) async-start(), calls=%async_computation.19 | async-start | bytes 16777216 | tf_op jit(solution)/shard_map/psum | solution.py:200
  187.3 952.3 %copy-start.44 = (f32[1024]{0:T(1024)}, f32[1024]{0:T(1024)S(1)}, u32[]{:S(2)}) copy-start(f32[1024]{0:T(1024)S(1)} %fusion.97) | copy-start | bytes 12292
  476.4 3.3 copy-start.3
  663.6 15.1 copy-start.46
  663.6 15.1 copy-start.49
  691.8 447.8 %all-reduce.7.cloned.1.call-start = ((), (), s32[]{:S(2)}) async-start(), calls=%async_computation.18 | async-start | bytes 8388608 | tf_op jit(solution)/shard_map/psum | solution.py:175
  705.6 596.5 %reduce-scatter.10.cloned.1.call-start = ((), (), s32[]{:S(2)}) async-start(), calls=%async_computation.20 | async-start | bytes 6291456 | tf_op jit(solution)/shard_map/reduce_scatter | solution.py:224
  1139.5 15.7 copy-start.48
  1151.9 3.4 copy-start.7
  1155.3 3.5 copy-start.2
  1155.3 3.5 copy-start.41
  1172.0 13.2 copy-start.8
  1200.1 7.5 copy-start
  1200.1 7.5 copy-start.12
  1207.6 3.7 copy-start.9
  1235.4 13.2 copy-start.8
  1263.5 8.7 copy-start
  1263.5 8.7 copy-start.12
  1272.2 3.7 copy-start.9
  1288.5 2.0 copy-start.20
  1288.5 3.0 copy-start.14
  1288.6 26.4 %reduce-scatter.12.cloned.1.call-start = ((), (), s32[]{:S(2)}) async-start(), calls=%async_computation.21 | async-start | bytes 6291456 | tf_op jit(solution)/shard_map/reduce_scatter | solution.py:225
  1289.1 332.7 %all-reduce.11.cloned.1.call-start = ((), (), s32[]{:S(2)}) async-start(), calls=%async_computation.22 | async-start | bytes 16777216 | tf_op jit(solution)/shard_map/psum | solution.py:250
  1293.7 2.0 copy-start.28
  1294.4 2.1 copy-start.31
  1302.1 2.2 copy-start.16
  1314.9 2.9 copy-start.15
  1329.6 346.2 %reduce-scatter.14.cloned.1.call-start = ((), (), s32[]{:S(2)}) async-start(), calls=%async_computation.23 | async-start | bytes 4718592 | tf_op jit(solution)/shard_map/reduce_scatter | solution.py:245
  1330.7 2.9 copy-start.5
  1330.7 2.9 copy-start.39
  1330.7 2.9 copy-start.43
  1338.8 391.9 %reduce-scatter.20.cloned.1.call-start = ((), (), s32[]{:S(2)}) async-start(), calls=%async_computation.26 | async-start | bytes 4718592 | tf_op jit(solution)/shard_map/reduce_scatter | solution.py:248
  1347.8 437.9 %reduce-scatter.16.cloned.1.call-start = ((), (), s32[]{:S(2)}) async-start(), calls=%async_computation.24 | async-start | bytes 4718592 | tf_op jit(solution)/shard_map/reduce_scatter | solution.py:246
  1356.0 484.8 %reduce-scatter.18.cloned.1.call-start = ((), (), s32[]{:S(2)}) async-start(), calls=%async_computation.25 | async-start | bytes 4718592 | tf_op jit(solution)/shard_map/reduce_scatter | solution.py:247
  1364.3 596.7 %reduce-scatter.22.cloned.1.call-start = ((), (), s32[]{:S(2)}) async-start(), calls=%async_computation.27 | async-start | bytes 18874368 | tf_op jit(solution)/shard_map/reduce_scatter | solution.py:196
  1379.7 701.7 %reduce-scatter.24.cloned.1.call-start = ((), (), s32[]{:S(2)}) async-start(), calls=%async_computation.28 | async-start | bytes 18874368 | tf_op jit(solution)/shard_map/reduce_scatter | solution.py:197
  1395.0 806.6 %reduce-scatter.26.cloned.1.call-start = ((), (), s32[]{:S(2)}) async-start(), calls=%async_computation.29 | async-start | bytes 18874368 | tf_op jit(solution)/shard_map/reduce_scatter | solution.py:198
  1621.8 6.8 copy-start.6
  1621.8 8.4 copy-start.11
  (14 other events, 17.5 us)
Sparse Core Ops, SparseCore 0:
  10.4 30.4 all-gather.12
  43.4 27.7 all-gather.16
  73.7 27.7 all-gather.10
  102.9 10.5 all-gather.14
  114.9 11.7 all-gather.26
  128.4 29.3 all-gather.18
  179.9 290.9 all-reduce.4
  473.4 53.2 all-gather.20
  529.1 54.2 all-gather.22
  585.7 55.8 all-gather.24
  691.9 290.8 all-reduce.8
  985.5 153.9 all-reduce.6
  1288.7 10.8 reduce-scatter.9
  1301.7 13.1 reduce-scatter.11
  1329.7 292.0 all-reduce.10
  1625.6 50.1 reduce-scatter.13
  1679.6 51.0 reduce-scatter.19
  1734.5 51.1 reduce-scatter.15
  1789.6 51.1 reduce-scatter.17
  1844.8 116.1 reduce-scatter.21
  1965.1 116.1 reduce-scatter.23
  2085.5 115.9 reduce-scatter.25
where the time goes:
time: 2220 us; the launch traced here: 2210 us
  waiting for transfers between devices  1680 us (76%)
  matrix products  326 us (15%)
  other arithmetic  127 us (6%)
  local copies, waits for them, and re-layouts  55.2 us (2%)
    psum x1, waiting for transfers between devices, body(): resid = tokens_wide + lax.psum(branch_part, 'tp')  284 us
    psum x1, waiting for transfers between devices, body(): grad_input_two = lax.psum(grad_input_two, 'tp')  277 us
    psum x1, waiting for transfers between devices, body(): grad_input_one = lax.psum(grad_input_one, 'tp')  211 us
    psum x1, waiting for transfers between devices, body(): lax.psum(branch_two_part.astype(jnp.bfloat16), 'tp').astype(jnp.float32)  150 us
    reduce_scatter x1, waiting for transfers between devices, body(): lax.psum_scatter(grad_up, ('shard', 'ctx'), scatter_dimension=0, tiled=True)  120 us
    reduce_scatter x1, waiting for transfers between devices, body(): lax.psum_scatter(grad_gate, ('shard', 'ctx'), scatter_dimension=0, tiled=...  120 us
    reduce_scatter x1, waiting for transfers between devices, body(): lax.psum_scatter(grad_down, ('shard', 'ctx'), scatter_dimension=1, tiled=...  120 us
    dot_general x7, matrix products, matmul_low(): return jnp.dot(left, right, preferred_element_type=jnp.float32)  68.5 us
  transfers between devices with their start and end apart: 22, of which 18 were waited for; matrix products, arithmetic and copies ran while one was open for 12% of the time, Pallas kernels for 0%

commit v1 on v0

--- a/solution.py
+++ b/solution.py
@@ -197,7 +197,11 @@
         lax.psum_scatter(grad_up, ("shard", "ctx"), scatter_dimension=0, tiled=True),
         lax.psum_scatter(grad_down, ("shard", "ctx"), scatter_dimension=1, tiled=True),
     )
-    grad_input_two = lax.psum(grad_input_two, "tp")
+    grad_input_two = grad_input_two
+    for hop in (1, 2):
+        grad_input_two = grad_input_two + lax.ppermute(
+            grad_input_two, "tp", [(dev, dev ^ hop) for dev in range(4)]
+        )
     grad_resid = grad_final + norm_back(normed_two, scale_two, grad_input_two)
     grad_resid_low = grad_resid.astype(bf_type)
     grad_wout = jnp.einsum(

time: 2220 us -> 2480 us (1.12)
  waiting for transfers between devices: 1680 us -> 1920 us
    ppermute x0 -> x2, waiting for transfers between devices: none -> 663 us  [body(): lax.ppermute(grad_input_two, 'tp', [(dev, dev ^ hop) for dev in range(4)])]
    psum x1 -> x0, waiting for transfers between devices: 277 us -> none  [body(): grad_input_two = lax.psum(grad_input_two, 'tp')]
    psum x1, waiting for transfers between devices: 150 us -> 0.01 us  [body(): lax.psum(branch_two_part.astype(jnp.bfloat16), 'tp').astype(jnp.float32)]
  transfers between devices with their start and end apart: 22 -> 23, of which waited for: 18 -> 18; matrix products, arithmetic and copies ran while one was open for 12% -> 11% of each run, Pallas kernels for 0% -> 0%
where the time goes in v1:
time: 2480 us; the launch traced here: 2470 us
  waiting for transfers between devices  1920 us (77%)
  matrix products  326 us (13%)
  other arithmetic  144 us (6%)
  local copies, waits for them, and re-layouts  58.8 us (2%)
    ppermute x2, waiting for transfers between devices, body(): lax.ppermute(grad_input_two, 'tp', [(dev, dev ^ hop) for dev in range(4)])  663 us
    psum x1, waiting for transfers between devices, body(): resid = tokens_wide + lax.psum(branch_part, 'tp')  284 us
    psum x1, waiting for transfers between devices, body(): grad_input_one = lax.psum(grad_input_one, 'tp')  210 us
    reduce_scatter x1, waiting for transfers between devices, body(): lax.psum_scatter(grad_up, ('shard', 'ctx'), scatter_dimension=0, tiled=True)  120 us
    reduce_scatter x1, waiting for transfers between devices, body(): lax.psum_scatter(grad_gate, ('shard', 'ctx'), scatter_dimension=0, tiled=...  120 us
    reduce_scatter x1, waiting for transfers between devices, body(): lax.psum_scatter(grad_down, ('shard', 'ctx'), scatter_dimension=1, tiled=...  120 us
    dot_general x7, matrix products, matmul_low(): return jnp.dot(left, right, preferred_element_type=jnp.float32)  69 us
    reduce_scatter x1, waiting for transfers between devices, body(): lax.psum_scatter(grad_wv, ('shard', 'ctx'), scatter_dimension=0, tiled=True)  55.1 us
  transfers between devices with their start and end apart: 23, of which 18 were waited for; matrix products, arithmetic and copies ran while one was open for 11% of the time, Pallas kernels for 0%

profile of v1, /device:TPU:0, one launch (start us, length us, event | category | flops | bytes accessed | tf_op | source)
XLA Modules:
  0.0 2470.1 jit_solution(3313978422236256612)
XLA Ops:
  21.9 19.1 all-gather.13.cloned.1.call-done
  41.0 5.2 fusion.107
  48.2 23.1 all-gather.17.cloned.1.call-done
  74.2 5.6 fusion.79
  83.5 18.1 all-gather.11.cloned.1.call-done
  101.5 6.6 fusion.106
  128.5 4.5 fusion.61
  136.1 35.1 %while.27 = (s32[]{:T(128)}, bf16[2,512,4,128]{3,2,1,0:T(4,128)(2,1)S(1)}, f32[2,4,512]{2,1,0:T(4,128)S(1)}, s32[2]{0:T(128)S(1)}, s32[]{:T(128)}, /*index=5*/s3...) while((s32[]{:T(128)}, ...), condition=%wide.region_5.6_spmd, body=%wide.region_2.5_spmd.sunk | while | flops 2195980800 | bytes 69280448 | solution.py:71
  139.2 4.5 fusion.170
  143.7 4.4 exponential_reduce_fusion.2
  148.1 5.3 fusion.171
  156.6 4.5 fusion.170
  161.0 4.4 exponential_reduce_fusion.2
  165.5 5.3 fusion.171
  171.3 8.4 fusion.87
  187.3 283.6 %all-reduce.4.cloned.1.call-done = f32[1024,2048]{1,0:T(8,128)} async-done(((f32[1024,2048]{1,0:T(8,128)}), f32[1024,2048]{1,0:T(8,128)}) %all-reduce.4.cloned.1.call-update) | async-done | bytes 8388624 | tf_op jit(solution)/shard_map/psum | solution.py:167
  470.9 5.5 fusion.104
  482.5 44.1 %all-gather.21.cloned.1.call-done = bf16[2048,2048]{1,0:T(8,128)(2,1)} async-done(((bf16[256,2048]{1,0:T(8,128)(2,1)}), bf16[2048,2048]{1,0:T(8,128)(2,1)}) %all-gather.21.cloned.1.call-update) | async-done | bytes 8388624 | tf_op jit(solution)/shard_map/all_gather | solution.py:140
  526.6 14.4 fusion.108
  541.1 42.3 %all-gather.23.cloned.1.call-done = bf16[2048,2048]{1,0:T(8,128)(2,1)} async-done(((bf16[256,2048]{1,0:T(8,128)(2,1)}), bf16[2048,2048]{1,0:T(8,128)(2,1)}) %all-gather.23.cloned.1.call-update) | async-done | bytes 8388624 | tf_op jit(solution)/shard_map/all_gather | solution.py:141
  583.4 14.5 fusion.109
  597.8 43.7 %all-gather.25.cloned.1.call-done = bf16[2048,2048]{1,0:T(8,128)(2,1)} async-done(((bf16[2048,256]{1,0:T(8,128)(2,1)}), bf16[2048,2048]{1,0:T(8,128)(2,1)}) %all-gather.25.cloned.1.call-update) | async-done | bytes 8388624 | tf_op jit(solution)/shard_map/all_gather | solution.py:142
  641.6 22.0 multiply_convert_fusion.1
  663.6 14.9 fusion.110
  678.5 12.8 convolution_add_fusion
  696.1 181.2 %collective-permute-done = f32[1024,2048]{1,0:T(8,128)} collective-permute-done((f32[1024,2048]{1,0:T(8,128)S(1)}, f32[1024,2048]{1,0:T(8,128)}, u32[]{:S(2)}, u32[]{:S(2)}) %collective-permute-start) | collective-permute-done | bytes 8388640 | tf_op jit(solution)/shard_map/ppermute | solution.py:202
  877.3 11.8 add.181
  891.5 14.2 convolution_convert_fusion
  905.8 481.6 %collective-permute-done.1 = f32[1024,2048]{1,0:T(8,128)} collective-permute-done((f32[1024,2048]{1,0:T(8,128)}, f32[1024,2048]{1,0:T(8,128)}, u32[]{:S(2)}, u32[]{:S(2)}) %collective-permute-start.1) | collective-permute-done | bytes 8388640 | tf_op jit(solution)/shard_map/ppermute | solution.py:202
  1387.3 12.4 fusion.103
  1399.7 12.3 fusion.46
  1412.1 3.4 copy-done.7
  1419.0 129.8 %while.28 = (s32[]{:T(128)}, f32[2048,4,128]{0,2,1:T(8,128)}, f32[2048,4,128]{0,2,1:T(8,128)}, f32[2,512,4,128]{3,1,2,0:T(8,128)}, bf16[2,512,4,128]{3,1,2,0:T(8...) while((s32[]{:T(128)}, f32[2048,4,128]{0,2,1:T(8,128)}, ...), condition=%wide.region_14.15_spmd.clone, body=%wide.region_12.14_spmd.clone.sunk | while | flops 5439226368 | bytes 211879280 | solution.py:107
  1419.2 9.2 fusion.180
  1432.3 13.1 multiply_reduce_fusion.4
  1445.4 14.9 multiply_convert_fusion.5
  1460.3 7.5 bitcast_add_fusion.4
  1471.5 11.1 bitcast_add_fusion.5
  1482.6 9.2 fusion.180
  1495.7 13.1 multiply_reduce_fusion.4
  1508.8 14.9 multiply_convert_fusion.5
  1523.8 8.7 bitcast_add_fusion.4
  1536.1 12.2 bitcast_add_fusion.5
  1556.8 5.6 fusion.82
  1566.3 6.2 fusion.111
  1572.6 3.8 reduce-scatter.12.cloned.1.call-done
  1579.2 11.8 add_add_fusion
  1595.1 5.2 fusion.54
  1601.5 7.7 fusion.68
  1609.3 15.2 fusion.112
  1624.8 15.3 fusion.113
  1640.7 15.4 fusion.72
  1657.4 7.2 fusion.52
  1665.9 7.0 fusion.56
  1672.9 210.3 %all-reduce.8.cloned.1.call-done = f32[1024,2048]{1,0:T(8,128)} async-done(((f32[1024,2048]{1,0:T(8,128)}), f32[1024,2048]{1,0:T(8,128)}) %all-reduce.8.cloned.1.call-update) | async-done | bytes 8388624 | tf_op jit(solution)/shard_map/psum | solution.py:254
  1883.3 6.6 fusion.102
  1891.6 7.5 fusion.42
  1899.2 38.1 %reduce-scatter.14.cloned.1.call-done = f32[256,512]{1,0:T(8,128)} async-done(((f32[2048,512]{1,0:T(8,128)}), f32[256,512]{1,0:T(8,128)}) %reduce-scatter.14.cloned.1.call-update) | async-done | bytes 524304 | tf_op jit(solution)/shard_map/reduce_scatter | solution.py:249
  1937.2 54.9 %reduce-scatter.20.cloned.1.call-done = f32[512,256]{1,0:T(8,128)} async-done(((f32[512,2048]{1,0:T(8,128)}), f32[512,256]{1,0:T(8,128)}) %reduce-scatter.20.cloned.1.call-update) | async-done | bytes 524304 | tf_op jit(solution)/shard_map/reduce_scatter | solution.py:252
  1992.1 120.2 %reduce-scatter.22.cloned.1.call-done = f32[256,2048]{1,0:T(8,128)} async-done(((f32[2048,2048]{1,0:T(8,128)}), f32[256,2048]{1,0:T(8,128)}) %reduce-scatter.22.cloned.1.call-update) | async-done | bytes 2097168 | tf_op jit(solution)/shard_map/reduce_scatter | solution.py:196
  2112.3 120.2 %reduce-scatter.24.cloned.1.call-done = f32[256,2048]{1,0:T(8,128)} async-done(((f32[2048,2048]{1,0:T(8,128)}), f32[256,2048]{1,0:T(8,128)}) %reduce-scatter.24.cloned.1.call-update) | async-done | bytes 2097168 | tf_op jit(solution)/shard_map/reduce_scatter | solution.py:197
  2232.5 120.2 %reduce-scatter.26.cloned.1.call-done = f32[2048,256]{1,0:T(8,128)} async-done(((f32[2048,2048]{1,0:T(8,128)}), f32[2048,256]{1,0:T(8,128)}) %reduce-scatter.26.cloned.1.call-update) | async-done | bytes 2097168 | tf_op jit(solution)/shard_map/reduce_scatter | solution.py:198
  2352.7 55.0 %reduce-scatter.16.cloned.1.call-done = f32[256,512]{1,0:T(8,128)} async-done(((f32[2048,512]{1,0:T(8,128)}), f32[256,512]{1,0:T(8,128)}) %reduce-scatter.16.cloned.1.call-update) | async-done | bytes 524304 | tf_op jit(solution)/shard_map/reduce_scatter | solution.py:250
  2407.7 55.1 %reduce-scatter.18.cloned.1.call-done = f32[256,512]{1,0:T(8,128)} async-done(((f32[2048,512]{1,0:T(8,128)}), f32[256,512]{1,0:T(8,128)}) %reduce-scatter.18.cloned.1.call-update) | async-done | bytes 524304 | tf_op jit(solution)/shard_map/reduce_scatter | solution.py:251
  (247 shorter events, 114.0 us)
Async XLA Ops:
  7.2 33.8 %all-gather.13.cloned.1.call-start = ((), (), s32[]{:S(2)}) async-start(), calls=%async_computation.10 | async-start | bytes 2359296 | tf_op jit(solution)/shard_map/all_gather | solution.py:135
  9.0 62.2 %all-gather.17.cloned.1.call-start = ((), (), s32[]{:S(2)}) async-start(), calls=%async_computation.12 | async-start | bytes 2359296 | tf_op jit(solution)/shard_map/all_gather | solution.py:136
  10.9 90.6 %all-gather.11.cloned.1.call-start = ((), (), s32[]{:S(2)}) async-start(), calls=%async_computation.9 | async-start | bytes 2359296 | tf_op jit(solution)/shard_map/all_gather | solution.py:134
  12.7 120.2 %all-gather.15.cloned.1.call-start = ((), (), s32[]{:S(2)}) async-start(), calls=%async_computation.11 | async-start | bytes 3145728 | tf_op jit(solution)/shard_map/all_gather | solution.py:156
  12.8 5.2 copy-start.4
  14.8 31.7 %copy-start.18 = (f32[1024,128]{0,1:T(8,128)}, f32[1024,128]{0,1:T(8,128)S(1)}, u32[]{:S(2)}) copy-start(f32[1024,128]{0,1:T(8,128)S(1)} %get-tuple-element.319) | copy-start | bytes 1572868
  14.8 31.7 %copy-start.20 = (f32[1024,128]{0,1:T(8,128)}, f32[1024,128]{0,1:T(8,128)S(1)}, u32[]{:S(2)}) copy-start(f32[1024,128]{0,1:T(8,128)S(1)} %get-tuple-element.320) | copy-start | bytes 1572868
  18.0 56.2 %copy-start.39 = (f32[1024]{0:T(1024)}, f32[1024]{0:T(1024)S(1)}, u32[]{:S(2)}) copy-start(f32[1024]{0:T(1024)S(1)} %broadcast_multiply_fusion.7) | copy-start | bytes 12292
  19.3 54.9 %copy-start.43 = (f32[1024]{0:T(1024)}, f32[1024]{0:T(1024)S(1)}, u32[]{:S(2)}) copy-start(f32[1024]{0:T(1024)S(1)} %add_rsqrt_fusion.1) | copy-start | bytes 12292
  48.1 87.9 %all-gather.27.cloned.1.call-start = ((), (), s32[]{:S(2)}) async-start(), calls=%async_computation.29 | async-start | bytes 3145728 | tf_op jit(solution)/shard_map/all_gather | solution.py:157
  74.2 5.7 copy-start.38
  79.9 91.4 %all-gather.19.cloned.1.call-start = ((), (), s32[]{:S(2)}) async-start(), calls=%async_computation.13 | async-start | bytes 2359296 | tf_op jit(solution)/shard_map/all_gather | solution.py:137
  80.7 390.2 %all-reduce.4.cloned.1.call-start = ((), (), s32[]{:S(2)}) async-start(), calls=%async_computation.14 | async-start | bytes 16777216 | tf_op jit(solution)/shard_map/psum | solution.py:167
  83.4 45.0 %copy-start.22 = (f32[2,512,128]{2,1,0:T(8,128)}, f32[2,512,128]{2,1,0:T(8,128)S(1)}, u32[]{:S(2)}) copy-start(f32[2,512,128]{2,1,0:T(8,128)S(1)} %get-tuple-element.317) | copy-start | bytes 1572868
  83.4 45.0 %copy-start.24 = (f32[2,512,128]{2,1,0:T(8,128)}, f32[2,512,128]{2,1,0:T(8,128)S(1)}, u32[]{:S(2)}) copy-start(f32[2,512,128]{2,1,0:T(8,128)S(1)} %get-tuple-element.318) | copy-start | bytes 1572868
  132.9 3.2 copy-start.35
  143.7 4.4 copy-start.10
  161.0 4.4 copy-start.10
  171.2 8.5 copy-start.1
  171.2 8.5 copy-start.36
  171.3 8.5 copy-start.41
  179.8 346.8 %all-gather.21.cloned.1.call-start = ((), (), s32[]{:S(2)}) async-start(), calls=%async_computation.15 | async-start | bytes 9437184 | tf_op jit(solution)/shard_map/all_gather | solution.py:140
  182.4 3.0 copy-start.31
  182.5 400.9 %all-gather.23.cloned.1.call-start = ((), (), s32[]{:S(2)}) async-start(), calls=%async_computation.16 | async-start | bytes 9437184 | tf_op jit(solution)/shard_map/all_gather | solution.py:141
  185.4 456.2 %all-gather.25.cloned.1.call-start = ((), (), s32[]{:S(2)}) async-start(), calls=%async_computation.17 | async-start | bytes 9437184 | tf_op jit(solution)/shard_map/all_gather | solution.py:142
  186.6 1213.2 %all-reduce.6.cloned.1.call-start = ((), (), s32[]{:S(2)}) async-start(), calls=%async_computation.18 | async-start | bytes 8388608 | tf_op jit(solution)/shard_map/psum | solution.py:175
  187.3 1212.5 %copy-start.45 = (f32[1024]{0:T(1024)}, f32[1024]{0:T(1024)S(1)}, u32[]{:S(2)}) copy-start(f32[1024]{0:T(1024)S(1)} %fusion.97) | copy-start | bytes 12292
  476.4 3.4 copy-start.3
  663.6 14.9 copy-start.49
  691.3 3.3 copy-start.15
  694.6 182.7 %collective-permute-start = (f32[1024,2048]{1,0:T(8,128)S(1)}, f32[1024,2048]{1,0:T(8,128)}, u32[]{:S(2)}, u32[]{:S(2)}) collective-permute-start(f32[1024,2048]{1,0:T(8,128)S(1)} %convolution_add_fusion), channel_id=1, source_target_pairs={{0,1},{1,0},{2,3},{3,2},{4,5},{5,4},{6,7},{7,6},{8,9},{9,8},{10,11... | collective-permute-start | bytes 25165832 | tf_op jit(solution)/shard_map/ppermute | solution.py:202
  889.1 498.3 %collective-permute-start.1 = (f32[1024,2048]{1,0:T(8,128)}, f32[1024,2048]{1,0:T(8,128)}, u32[]{:S(2)}, u32[]{:S(2)}) collective-permute-start(f32[1024,2048]{1,0:T(8,128)} %add.181), channel_id=1, source_target_pairs={{0,2},{1,3},{2,0},{3,1},{4,6},{5,7},{6,4},{7,5},{8,10},{9,11},{10,... | collective-permute-start | bytes 25165832 | tf_op jit(solution)/shard_map/ppermute | solution.py:202
  905.7 656.7 %reduce-scatter.10.cloned.1.call-start = ((), (), s32[]{:S(2)}) async-start(), calls=%async_computation.19 | async-start | bytes 6291456 | tf_op jit(solution)/shard_map/reduce_scatter | solution.py:228
  1399.7 15.7 copy-start.48
  1412.1 3.4 copy-start.7
  1415.5 3.5 copy-start.2
  1415.5 3.5 copy-start.42
  1432.3 13.1 copy-start.8
  1460.3 7.5 copy-start
  1460.3 7.5 copy-start.12
  1467.8 3.7 copy-start.9
  1495.7 13.2 copy-start.8
  1523.8 8.7 copy-start
  1523.8 8.7 copy-start.12
  1532.4 3.7 copy-start.9
  1548.8 2.0 copy-start.21
  1548.8 3.0 copy-start.14
  1548.8 27.5 %reduce-scatter.12.cloned.1.call-start = ((), (), s32[]{:S(2)}) async-start(), calls=%async_computation.20 | async-start | bytes 6291456 | tf_op jit(solution)/shard_map/reduce_scatter | solution.py:229
  1549.6 333.7 %all-reduce.8.cloned.1.call-start = ((), (), s32[]{:S(2)}) async-start(), calls=%async_computation.21 | async-start | bytes 16777216 | tf_op jit(solution)/shard_map/psum | solution.py:254
  1554.6 2.1 copy-start.32
  1562.4 2.2 copy-start.17
  1576.3 2.9 copy-start.16
  1591.0 346.2 %reduce-scatter.14.cloned.1.call-start = ((), (), s32[]{:S(2)}) async-start(), calls=%async_computation.22 | async-start | bytes 4718592 | tf_op jit(solution)/shard_map/reduce_scatter | solution.py:249
  1592.2 2.9 copy-start.5
  1592.2 2.9 copy-start.40
  1592.2 2.9 copy-start.44
  1600.3 391.8 %reduce-scatter.20.cloned.1.call-start = ((), (), s32[]{:S(2)}) async-start(), calls=%async_computation.25 | async-start | bytes 4718592 | tf_op jit(solution)/shard_map/reduce_scatter | solution.py:252
  1609.2 503.1 %reduce-scatter.22.cloned.1.call-start = ((), (), s32[]{:S(2)}) async-start(), calls=%async_computation.26 | async-start | bytes 18874368 | tf_op jit(solution)/shard_map/reduce_scatter | solution.py:196
  1624.5 608.0 %reduce-scatter.24.cloned.1.call-start = ((), (), s32[]{:S(2)}) async-start(), calls=%async_computation.27 | async-start | bytes 18874368 | tf_op jit(solution)/shard_map/reduce_scatter | solution.py:197
  1640.1 712.6 %reduce-scatter.26.cloned.1.call-start = ((), (), s32[]{:S(2)}) async-start(), calls=%async_computation.28 | async-start | bytes 18874368 | tf_op jit(solution)/shard_map/reduce_scatter | solution.py:198
  1656.2 751.5 %reduce-scatter.16.cloned.1.call-start = ((), (), s32[]{:S(2)}) async-start(), calls=%async_computation.23 | async-start | bytes 4718592 | tf_op jit(solution)/shard_map/reduce_scatter | solution.py:250
  1664.6 798.2 %reduce-scatter.18.cloned.1.call-start = ((), (), s32[]{:S(2)}) async-start(), calls=%async_computation.24 | async-start | bytes 4718592 | tf_op jit(solution)/shard_map/reduce_scatter | solution.py:251
  1883.3 6.7 copy-start.6
  1883.3 8.4 copy-start.11
  (15 other events, 19.6 us)
Sparse Core Ops, SparseCore 0:
  10.4 30.4 all-gather.12
  43.4 27.7 all-gather.16
  73.7 27.7 all-gather.10
  102.9 10.5 all-gather.14
  114.9 11.7 all-gather.26
  128.4 29.2 all-gather.18
  179.9 290.9 all-reduce.3
  473.4 53.2 all-gather.20
  529.1 54.2 all-gather.22
  585.7 55.8 all-gather.24
  905.8 380.9 all-reduce.5
  1548.9 11.8 reduce-scatter.9
  1563.1 13.1 reduce-scatter.11
  1591.2 292.0 all-reduce.7
  1887.0 50.1 reduce-scatter.13
  1941.0 51.0 reduce-scatter.19
  1996.1 116.1 reduce-scatter.21
  2116.3 116.1 reduce-scatter.23
  2236.7 116.0 reduce-scatter.25
  2356.5 51.1 reduce-scatter.15
  2411.6 51.1 reduce-scatter.17
